TPU v7x, 32 devices: a whole 2x2x4 slice. The times are simulated.
32 devices in a mesh: grp: 8 (over z, x), sp: 4 (over y, core).
Axes of the slice: x: 2, y: 2, z: 4, core: 2. Of those that a mesh axis runs over, the one named last changes fastest.
Arguments:
- query_rows: bfloat16 [4096, 4096], P(('grp', 'sp')), parts along dimension 0, may hold values from -250 to 250
- key_rows: bfloat16 [4096, 1024], P(('grp', 'sp')), parts along dimension 0, may hold values from -4 to 4
- value_rows: bfloat16 [4096, 1024], P(('grp', 'sp')), parts along dimension 0, may hold values from -6 to 6
- out_grad: bfloat16 [4096, 4096], P(('grp', 'sp')), parts along dimension 0, may hold values from -6 to 6
- question_lengths: int32 [64], P('grp'), parts along dimension 0, may hold values from 1 to 128, 256 in all
Outputs:
- query_grad: bfloat16 [4096, 4096], P(('grp', 'sp')), parts along dimension 0
- key_grad: bfloat16 [4096, 1024], P(('grp', 'sp')), parts along dimension 0
- value_grad: bfloat16 [4096, 1024], P(('grp', 'sp')), parts along dimension 0
There are 8 independent parts, one for each index of `grp`. A program takes and returns all parts, laid end to end along the dimension named above; each array names one. Nothing has to cross between parts.
All inputs are finite; a program needn't handle non-finite values.
Results may differ from a plain program's by a relative error of at most 0.033.
Values may be sent and summed in bfloat16 or wider, within the bound.
No kernel may reach another device: no remote copies, remote signals or barrier semaphores. Data moves between devices by JAX's collectives and lax.ppermute only.
A program may use at most 128 MiB of HBM per device.

v0:
```python
from functools import partial
from functools import reduce
import math
import jax
import jax.numpy as jnp
from jax import lax
from jax.sharding import PartitionSpec as P

HD = 128
QH = 32
KVH = 8
MASKED = -1e30


def widen(rows, copies):
    tokens = rows.shape[0]
    shaped = rows.reshape(tokens, KVH, 1, HD)
    return jnp.broadcast_to(shaped, (tokens, KVH, copies, HD)).reshape(tokens, KVH * copies * HD)


def segment_ids(question_lengths, length, doc_len):
    ends = jnp.cumsum(question_lengths)
    places = jnp.arange(length, dtype=jnp.int32)
    inside = jnp.sum((ends[None, :] <= (places - doc_len)[:, None]).astype(jnp.int32), axis=1)
    return jnp.where(places < doc_len, -1, inside)


def make_scores(query_block, key_block, visible, scaling):
    raw = (
        jnp.einsum("bkgd,skd->kgbs", query_block, key_block, preferred_element_type=jnp.float32)
        * scaling
    )
    return jnp.where(visible[None, None], raw, MASKED)


def weighted_values(probs_b, value_block):
    return jnp.einsum("kgbs,skd->bkgd", probs_b, value_block, preferred_element_type=jnp.float32)


def backward_block(probs, probs_b, delta, grad_block, query_block, key_block, value_block, scaling):
    value_part = jnp.einsum(
        "kgbs,bkgd->skd", probs_b, grad_block, preferred_element_type=jnp.float32
    )
    prob_grad = jnp.einsum(
        "bkgd,skd->kgbs", grad_block, value_block, preferred_element_type=jnp.float32
    )
    score_grad = (probs * (prob_grad - delta[..., None])).astype(jnp.bfloat16)
    query_part = jnp.einsum(
        "kgbs,skd->bkgd", score_grad, key_block, preferred_element_type=jnp.float32
    )
    key_part = (
        jnp.einsum("kgbs,bkgd->skd", score_grad, query_block, preferred_element_type=jnp.float32)
        * scaling
    )
    return (query_part, key_part, value_part)


def on_device(query_rows, key_rows, value_rows, out_grad, question_lengths):
    devices = lax.axis_size("sp")
    tokens = query_rows.shape[0]
    length = tokens * devices
    doc_len = length // 2
    block_len = min(512, length)
    block_count = length // block_len
    scaling = 1.0 / math.sqrt(HD)
    copies = max(KVH, devices) // KVH
    keys_local, values_local = (
        lax.all_to_all(widen(key_rows, copies), "sp", split_axis=1, concat_axis=0, tiled=True),
        lax.all_to_all(widen(value_rows, copies), "sp", split_axis=1, concat_axis=0, tiled=True),
    )
    queries_local, grads_local = (
        lax.all_to_all(query_rows, "sp", split_axis=1, concat_axis=0, tiled=True),
        lax.all_to_all(out_grad, "sp", split_axis=1, concat_axis=0, tiled=True),
    )
    key_heads = KVH * copies // devices
    per_group = QH // devices // key_heads
    queries = queries_local.reshape(length, key_heads, per_group, HD)
    grads = grads_local.reshape(length, key_heads, per_group, HD)
    keys = keys_local.reshape(length, key_heads, HD)
    values = values_local.reshape(length, key_heads, HD)
    segment = segment_ids(question_lengths, length, doc_len)
    places = jnp.arange(length, dtype=jnp.int32)
    query_shape = (block_len, key_heads, per_group, HD)
    key_shape = (block_len, key_heads, HD)
    key_sums = [jnp.zeros(key_shape, jnp.float32)] * block_count
    value_sums = [jnp.zeros(key_shape, jnp.float32)] * block_count
    query_parts = []
    for row_block in range(block_count):
        row_start = row_block * block_len
        query_block = queries[row_start : row_start + block_len]
        grad_block = grads[row_start : row_start + block_len]
        row_places = places[row_start : row_start + block_len]
        row_segment = segment[row_start : row_start + block_len]
        needs = []
        scores = []
        for col_block in range(row_block + 1):
            col_start = col_block * block_len
            col_places = places[col_start : col_start + block_len]
            col_segment = segment[col_start : col_start + block_len]
            visible = (col_places[None, :] <= row_places[:, None]) & (
                (col_places[None, :] < doc_len) | (col_segment[None, :] == row_segment[:, None])
            )
            needed = True
            needs.append(needed)
            scores.append(
                make_scores(query_block, keys[col_start : col_start + block_len], visible, scaling)
            )
        peak = reduce(jnp.maximum, [jnp.max(score, axis=3) for score in scores])
        total = reduce(
            jnp.add, [jnp.sum(jnp.exp(score - peak[..., None]), axis=3) for score in scores]
        )
        log_total = peak + jnp.log(total)
        probs = [jnp.exp(score - log_total[..., None]) for score in scores]
        probs_low = [single.astype(jnp.bfloat16) for single in probs]
        output = jnp.zeros(query_shape, jnp.float32)
        for col_block in range(row_block + 1):
            col_start = col_block * block_len
            output = output + weighted_values(
                probs_low[col_block], values[col_start : col_start + block_len]
            )
        output_low = output.astype(jnp.bfloat16)
        delta = jnp.einsum(
            "bkgd,bkgd->kgb", grad_block, output_low, preferred_element_type=jnp.float32
        )
        query_sum = jnp.zeros(query_shape, jnp.float32)
        for col_block in range(row_block + 1):
            col_start = col_block * block_len
            action = partial(
                backward_block,
                probs[col_block],
                probs_low[col_block],
                delta,
                grad_block,
                query_block,
                keys[col_start : col_start + block_len],
                values[col_start : col_start + block_len],
                scaling,
            )
            query_part, key_part, value_part = action()
            query_sum = query_sum + query_part
            key_sums[col_block] = key_sums[col_block] + key_part
            value_sums[col_block] = value_sums[col_block] + value_part
        query_parts.append((query_sum * scaling).astype(jnp.bfloat16))
    query_local = jnp.concatenate(query_parts, axis=0).reshape(length, key_heads * per_group * HD)
    key_local = jnp.concatenate(key_sums, axis=0).reshape(length, key_heads * HD)
    value_local = jnp.concatenate(value_sums, axis=0).reshape(length, key_heads * HD)
    query_grad = lax.all_to_all(query_local, "sp", split_axis=0, concat_axis=1, tiled=True)
    key_back, value_back = (
        lax.all_to_all(key_local, "sp", split_axis=0, concat_axis=1, tiled=True),
        lax.all_to_all(value_local, "sp", split_axis=0, concat_axis=1, tiled=True),
    )
    key_grad = (
        jnp.sum(key_back.reshape(tokens, KVH, copies, HD), axis=2)
        .reshape(tokens, KVH * HD)
        .astype(jnp.bfloat16)
    )
    value_grad = (
        jnp.sum(value_back.reshape(tokens, KVH, copies, HD), axis=2)
        .reshape(tokens, KVH * HD)
        .astype(jnp.bfloat16)
    )
    return (query_grad, key_grad, value_grad)


def solution(mesh):
    return jax.shard_map(
        on_device,
        mesh=mesh,
        in_specs=(
            P(("grp", "sp"), None),
            P(("grp", "sp"), None),
            P(("grp", "sp"), None),
            P(("grp", "sp"), None),
            P("grp"),
        ),
        out_specs=(P(("grp", "sp"), None), P(("grp", "sp"), None), P(("grp", "sp"), None)),
        check_vma=False,
    )
```

profile of v0, /device:TPU:0, one launch (start us, length us, event | category | flops | bytes accessed | tf_op | source)
XLA Modules:
  0.0 117.2 jit_solution(11566615232329075632)
XLA Ops:
  0.6 1.7 %copy.125 = bf16[16,4,8,256]{3,2,0,1:T(8,128)(2,1)} copy(bf16[16,4,8,256]{3,2,1,0:T(8,128)(2,1)} %bitcast.94) | data formatting | bytes 524288 | tf_op jit(solution)/shard_map/all_to_all | solution.py:68
  2.3 4.3 %all-to-all-start = ((bf16[128,4,256]{2,0,1:T(8,128)(2,1)}), bf16[128,4,256]{2,0,1:T(8,128)(2,1)S(1)}, u32[]{:S(2)}, u32[]{:S(2)}) async-start(bf16[128,4,256]{2,0,1:T(8,128)(2,1)} %bitcast.76), calls=%async_computation | async-start | bytes 524288 | tf_op jit(solution)/shard_map/all_to_all | solution.py:68
  6.6 1.7 %copy.124 = bf16[16,4,8,256]{3,2,0,1:T(8,128)(2,1)} copy(bf16[16,4,8,256]{3,2,1,0:T(8,128)(2,1)} %bitcast.95) | data formatting | bytes 524288 | tf_op jit(solution)/shard_map/all_to_all | solution.py:69
  8.2 4.3 %all-to-all-done = bf16[128,4,256]{2,0,1:T(8,128)(2,1)S(1)} async-done(((bf16[128,4,256]{2,0,1:T(8,128)(2,1)}), bf16[128,4,256]{2,0,1:T(8,128)(2,1)S(1)}, u32[]{:S(2)}, u32[]{:S(2)}) %all-to-all-start) | async-done | bytes 262176 | tf_op jit(solution)/shard_map/all_to_all | solution.py:68
  12.6 3.4 %all-to-all-start.2 = ((bf16[128,4,256]{2,0,1:T(8,128)(2,1)}), bf16[128,4,256]{2,0,1:T(8,128)(2,1)S(1)}, u32[]{:S(2)}, u32[]{:S(2)}) async-start(bf16[128,4,256]{2,0,1:T(8,128)(2,1)} %bitcast.75), calls=%async_computation.2 | async-start | bytes 524288 | tf_op jit(solution)/shard_map/all_to_all | solution.py:69
  16.0 2.3 %copy.123 = bf16[16,4,8,1024]{3,2,0,1:T(8,128)(2,1)} copy(bf16[16,4,8,1024]{3,2,1,0:T(8,128)(2,1)} %bitcast.84) | data formatting | bytes 2097152 | tf_op jit(solution)/shard_map/all_to_all | solution.py:72
  18.3 3.7 %all-to-all-done.2 = bf16[128,4,256]{2,0,1:T(8,128)(2,1)S(1)} async-done(((bf16[128,4,256]{2,0,1:T(8,128)(2,1)}), bf16[128,4,256]{2,0,1:T(8,128)(2,1)S(1)}, u32[]{:S(2)}, u32[]{:S(2)}) %all-to-all-start.2) | async-done | bytes 262176 | tf_op jit(solution)/shard_map/all_to_all | solution.py:69
  22.0 3.5 %all-to-all-start.1 = ((bf16[128,4,1024]{2,0,1:T(8,128)(2,1)}), bf16[128,4,1024]{2,0,1:T(8,128)(2,1)S(1)}, u32[]{:S(2)}, u32[]{:S(2)}) async-start(bf16[128,4,1024]{2,0,1:T(8,128)(2,1)} %bitcast.74), calls=%async_computation.1 | async-start | bytes 2097152 | tf_op jit(solution)/shard_map/all_to_all | solution.py:72
  25.5 2.3 %copy.122 = bf16[16,4,8,1024]{3,2,0,1:T(8,128)(2,1)} copy(bf16[16,4,8,1024]{3,2,1,0:T(8,128)(2,1)} %bitcast.85) | data formatting | bytes 2097152 | tf_op jit(solution)/shard_map/all_to_all | solution.py:73
  28.0 11.9 %all-to-all-done.1 = bf16[128,4,1024]{2,0,1:T(8,128)(2,1)S(1)} async-done(((bf16[128,4,1024]{2,0,1:T(8,128)(2,1)}), bf16[128,4,1024]{2,0,1:T(8,128)(2,1)S(1)}, u32[]{:S(2)}, u32[]{:S(2)}) %all-to-all-start.1) | async-done | bytes 1048608 | tf_op jit(solution)/shard_map/all_to_all | solution.py:72
  39.9 3.5 %all-to-all-start.3 = ((bf16[128,4,1024]{2,0,1:T(8,128)(2,1)}), bf16[128,4,1024]{2,0,1:T(8,128)(2,1)S(1)}, u32[]{:S(2)}, u32[]{:S(2)}) async-start(bf16[128,4,1024]{2,0,1:T(8,128)(2,1)} %bitcast.73), calls=%async_computation.3 | async-start | bytes 2097152 | tf_op jit(solution)/shard_map/all_to_all | solution.py:73
  46.1 11.8 %all-to-all-done.3 = bf16[128,4,1024]{2,0,1:T(8,128)(2,1)S(1)} async-done(((bf16[128,4,1024]{2,0,1:T(8,128)(2,1)}), bf16[128,4,1024]{2,0,1:T(8,128)(2,1)S(1)}, u32[]{:S(2)}, u32[]{:S(2)}) %all-to-all-start.3) | async-done | bytes 1048608 | tf_op jit(solution)/shard_map/all_to_all | solution.py:73
  58.6 2.6 %fusion.3 = (f32[2,4,512]{2,1,0:T(4,128)S(1)}, f32[2,512,512,4]{2,1,3,0:T(8,128)S(1)}) fusion(pred[512,512]{0,1:T(8,128)(4,1)S(1)} %fusion.8, bf16[512,2,4,128]{3,2,1,0:T(4,128)(2,1)S(1)} %reshape.174, bf16[512,2,128,1]{2,1,0,3:T(2,128)(2,1)} %bitcast.92), kind=kOutput, calls=%fused_computation.7 | convolution fusion | flops 543158272 | bytes 9977856 | tf_op jit(solution)/shard_map/bkgd,skd->kgbs/dot_general | solution.py:30
  61.2 1.8 %exponential_reduce_fusion = f32[2,4,512]{2,1,0:T(4,128)S(1)} fusion(f32[2,512,512,4]{2,1,3,0:T(8,128)S(1)} %get-tuple-element.10, f32[2,4,512]{2,1,0:T(4,128)S(1)} %get-tuple-element.9, pred[512,512]{0,1:T(8,128)(4,1)S(1)} %fusion.8), kind=kLoop, calls=%fused_computation.5 | loop fusion | flops 8384512 | bytes 8683520 | tf_op jit(solution)/shard_map/reduce_sum | solution.py:110
  63.0 2.1 %convolution_bitcast_fusion = bf16[512,2,128]{2,0,1:T(8,128)(2,1)S(1)} fusion(bf16[512,2,4,128]{3,2,1,0:T(4,128)(2,1)S(1)} %reshape.176, f32[2,512,512,4]{2,1,3,0:T(8,128)S(1)} %get-tuple-element.10, f32[2,4,512]{2,1,0:T(4,128)S(1)} %bitcast.100, pred[512,512]{0,1:T(8,128)(4,1)S(1)} %fusion.8), kind=kOutput, calls=%fused_computation.13 | convolution fusion | flops 545259520 | bytes 9977856 | tf_op jit(solution)/shard_map/kgbs,bkgd->skd/dot_general | solution.py:41
  66.3 3.6 %all-to-all-start.6 = ((bf16[4,128,256]{2,1,0:T(8,128)(2,1)}), bf16[4,128,256]{2,1,0:T(8,128)(2,1)S(1)}, u32[]{:S(2)}, u32[]{:S(2)}) async-start(bf16[4,128,256]{2,1,0:T(8,128)(2,1)} %all_to_all.100), calls=%async_computation.6 | async-start | bytes 524288 | tf_op jit(solution)/shard_map/all_to_all | solution.py:150
  69.9 5.9 %fusion.4 = f32[2,4,512,128]{3,2,1,0:T(8,128)S(1)} fusion(bf16[512,2,128,1]{2,1,0,3:T(2,128)(2,1)S(1)} %bitcast.96, f32[2,512,512,4]{2,1,3,0:T(8,128)} %copy-done, f32[2,4,512]{2,1,0:T(4,128)S(1)} %bitcast.101, pred[512,512]{0,1:T(8,128)(4,1)S(1)} %fusion.8), kind=kOutput, calls=%fused_computation.11 | convolution fusion | flops 546308096 | bytes 11026432 | tf_op jit(solution)/shard_map/kgbs,skd->bkgd/dot_general | solution.py:37
  75.8 2.1 %multiply_reduce_fusion = f32[2,4,512]{1,0,2:T(2,128)S(1)} fusion(f32[2,4,512,128]{3,2,1,0:T(8,128)S(1)} %fusion.4, bf16[512,2,4,128]{3,2,1,0:T(4,128)(2,1)S(1)} %reshape.176), kind=kLoop, calls=%fused_computation.8 | loop fusion | flops 1568768 | bytes 3162112
  78.1 5.1 %fusion.1 = bf16[2,4,512,512]{2,3,1,0:T(8,128)(2,1)S(1)} fusion(f32[2,512,512,4]{2,1,3,0:T(8,128)} %copy-done, f32[2,4,512]{2,1,0:T(4,128)S(1)} %copy.80, f32[2,4,512]{2,1,0:T(4,128)S(1)} %bitcast.102, pred[512,512]{0,1:T(8,128)(4,1)S(1)} %fusion.8, bf16[512,2,4,128]{3,2,1,0:T(4,128)(2,1)S(1)} %reshape.176, bf16[512,2,128,1]{2,1,0,3:T(2,128)(2,1)S(1)} %bitcast.97), kind=kOutput, calls=%fused_computation.2 | convolution fusion | flops 549453824 | bytes 14188544 | tf_op jit(solution)/shard_map/bkgd,skd->kgbs/dot_general | solution.py:44
  83.2 1.9 %copy-done.1 = bf16[2,4,512,512]{2,3,1,0:T(8,128)(2,1)} copy-done((bf16[2,4,512,512]{2,3,1,0:T(8,128)(2,1)}, bf16[2,4,512,512]{2,3,1,0:T(8,128)(2,1)S(1)}, u32[]{:S(2)}) %copy-start.1) | copy-done | bytes 4194328
  87.6 3.4 %all-to-all-start.5 = ((bf16[4,128,256]{2,1,0:T(8,128)(2,1)}), bf16[4,128,256]{2,1,0:T(8,128)(2,1)S(1)}, u32[]{:S(2)}, u32[]{:S(2)}) async-start(bf16[4,128,256]{2,1,0:T(8,128)(2,1)} %all_to_all.98), calls=%async_computation.5 | async-start | bytes 524288 | tf_op jit(solution)/shard_map/all_to_all | solution.py:149
  91.0 3.9 %fusion.5 = bf16[512,2,4,128]{3,0,2,1:T(8,128)(2,1)S(1)} fusion(bf16[2,4,512,512]{2,3,1,0:T(8,128)(2,1)} %copy-done.1, bf16[512,2,128,1]{2,1,0,3:T(2,128)(2,1)S(1)} %bitcast.93), kind=kOutput, calls=%fused_computation.12 | convolution fusion | flops 537919488 | bytes 5505024 | tf_op jit(solution)/shard_map/kgbs,skd->bkgd/dot_general | solution.py:48
  97.3 3.5 %all-to-all-start.4 = ((bf16[4,128,1024]{2,1,0:T(8,128)(2,1)}), bf16[4,128,1024]{2,1,0:T(8,128)(2,1)S(1)}, u32[]{:S(2)}, u32[]{:S(2)}) async-start(bf16[4,128,1024]{2,1,0:T(8,128)(2,1)} %all_to_all.94), calls=%async_computation.4 | async-start | bytes 2097152 | tf_op jit(solution)/shard_map/all_to_all | solution.py:147
  102.9 12.3 %all-to-all-done.4 = bf16[4,128,1024]{2,1,0:T(8,128)(2,1)S(1)} async-done(((bf16[4,128,1024]{2,1,0:T(8,128)(2,1)}), bf16[4,128,1024]{2,1,0:T(8,128)(2,1)S(1)}, u32[]{:S(2)}, u32[]{:S(2)}) %all-to-all-start.4) | async-done | bytes 1048608 | tf_op jit(solution)/shard_map/all_to_all | solution.py:147
  (36 shorter events, 13.7 us)
Async XLA Ops:
  0.6 27.2 %copy-start.4 = (s32[8]{0:T(128)S(1)}, s32[8]{0:T(128)}, u32[]{:S(2)}) copy-start(s32[8]{0:T(128)} %param.9) | copy-start | bytes 100
  2.3 10.3 %all-to-all-start = ((bf16[128,4,256]{2,0,1:T(8,128)(2,1)}), bf16[128,4,256]{2,0,1:T(8,128)(2,1)S(1)}, u32[]{:S(2)}, u32[]{:S(2)}) async-start(bf16[128,4,256]{2,0,1:T(8,128)(2,1)} %bitcast.76), calls=%async_computation | async-start | bytes 524288 | tf_op jit(solution)/shard_map/all_to_all | solution.py:68
  12.6 9.4 %all-to-all-start.2 = ((bf16[128,4,256]{2,0,1:T(8,128)(2,1)}), bf16[128,4,256]{2,0,1:T(8,128)(2,1)S(1)}, u32[]{:S(2)}, u32[]{:S(2)}) async-start(bf16[128,4,256]{2,0,1:T(8,128)(2,1)} %bitcast.75), calls=%async_computation.2 | async-start | bytes 524288 | tf_op jit(solution)/shard_map/all_to_all | solution.py:69
  22.0 17.9 %all-to-all-start.1 = ((bf16[128,4,1024]{2,0,1:T(8,128)(2,1)}), bf16[128,4,1024]{2,0,1:T(8,128)(2,1)S(1)}, u32[]{:S(2)}, u32[]{:S(2)}) async-start(bf16[128,4,1024]{2,0,1:T(8,128)(2,1)} %bitcast.74), calls=%async_computation.1 | async-start | bytes 2097152 | tf_op jit(solution)/shard_map/all_to_all | solution.py:72
  39.9 17.9 %all-to-all-start.3 = ((bf16[128,4,1024]{2,0,1:T(8,128)(2,1)}), bf16[128,4,1024]{2,0,1:T(8,128)(2,1)S(1)}, u32[]{:S(2)}, u32[]{:S(2)}) async-start(bf16[128,4,1024]{2,0,1:T(8,128)(2,1)} %bitcast.73), calls=%async_computation.3 | async-start | bytes 2097152 | tf_op jit(solution)/shard_map/all_to_all | solution.py:73
  61.2 3.9 %copy-start = (f32[2,512,512,4]{2,1,3,0:T(8,128)}, f32[2,512,512,4]{2,1,3,0:T(8,128)S(1)}, u32[]{:S(2)}) copy-start(f32[2,512,512,4]{2,1,3,0:T(8,128)S(1)} %get-tuple-element.10) | copy-start | bytes 25165828
  63.0 6.9 %copy-start.3 = (bf16[512,2,128]{2,1,0:T(2,128)(2,1)S(1)}, bf16[512,2,128]{2,1,0:T(2,128)(2,1)}, u32[]{:S(2)}) copy-start(bf16[512,2,128]{2,1,0:T(2,128)(2,1)} %reshape.175) | copy-start | bytes 786436
  66.3 21.3 %all-to-all-start.6 = ((bf16[4,128,256]{2,1,0:T(8,128)(2,1)}), bf16[4,128,256]{2,1,0:T(8,128)(2,1)S(1)}, u32[]{:S(2)}, u32[]{:S(2)}) async-start(bf16[4,128,256]{2,1,0:T(8,128)(2,1)} %all_to_all.100), calls=%async_computation.6 | async-start | bytes 524288 | tf_op jit(solution)/shard_map/all_to_all | solution.py:150
  78.1 12.9 %copy-start.2 = (bf16[512,2,128]{2,1,0:T(2,128)(2,1)S(1)}, bf16[512,2,128]{2,1,0:T(2,128)(2,1)}, u32[]{:S(2)}) copy-start(bf16[512,2,128]{2,1,0:T(2,128)(2,1)} %reshape.173) | copy-start | bytes 786436
  83.2 1.9 %copy-start.1 = (bf16[2,4,512,512]{2,3,1,0:T(8,128)(2,1)}, bf16[2,4,512,512]{2,3,1,0:T(8,128)(2,1)S(1)}, u32[]{:S(2)}) copy-start(bf16[2,4,512,512]{2,3,1,0:T(8,128)(2,1)S(1)} %fusion.1) | copy-start | bytes 12582916
  87.6 9.7 %all-to-all-start.5 = ((bf16[4,128,256]{2,1,0:T(8,128)(2,1)}), bf16[4,128,256]{2,1,0:T(8,128)(2,1)S(1)}, u32[]{:S(2)}, u32[]{:S(2)}) async-start(bf16[4,128,256]{2,1,0:T(8,128)(2,1)} %all_to_all.98), calls=%async_computation.5 | async-start | bytes 524288 | tf_op jit(solution)/shard_map/all_to_all | solution.py:149
  97.3 17.9 %all-to-all-start.4 = ((bf16[4,128,1024]{2,1,0:T(8,128)(2,1)}), bf16[4,128,1024]{2,1,0:T(8,128)(2,1)S(1)}, u32[]{:S(2)}, u32[]{:S(2)}) async-start(bf16[4,128,1024]{2,1,0:T(8,128)(2,1)} %all_to_all.94), calls=%async_computation.4 | async-start | bytes 2097152 | tf_op jit(solution)/shard_map/all_to_all | solution.py:147
where the time goes:
time: 118 us; the launch traced here: 117 us
  waiting for transfers between devices  44 us (37%)
  starting transfers between devices  25.2 us (21%)
  local copies, waits for them, and re-layouts  21.7 us (18%)
  matrix products  21 us (18%)
  other arithmetic  4.36 us (4%)
    all_to_all x1, waiting for transfers between devices, on_device(): lax.all_to_all(query_local, 'sp', split_axis=0, concat_axis=1, tiled=True)  12.3 us
    all_to_all x1, waiting for transfers between devices, on_device(): lax.all_to_all(query_rows, 'sp', split_axis=1, concat_axis=0, tiled=True)  11.9 us
    all_to_all x1, waiting for transfers between devices, on_device(): lax.all_to_all(out_grad, 'sp', split_axis=1, concat_axis=0, tiled=True)  11.8 us
    dot_general x1, matrix products, weighted_values(): jnp.einsum('kgbs,skd->bkgd', probs_b, value_block, preferred_element_type...  5.91 us
    dot_general x1, matrix products, backward_block(): jnp.einsum('bkgd,skd->kgbs', grad_block, value_block, preferred_element_t...  5.15 us
    unnamed x13, local copies, waits for them, and re-layouts  4.96 us
    all_to_all x1, waiting for transfers between devices, on_device(): lax.all_to_all(widen(key_rows, copies), 'sp', split_axis=1, concat_axis=0...  4.34 us
    all_to_all x1, starting transfers between devices, on_device(): lax.all_to_all(widen(key_rows, copies), 'sp', split_axis=1, concat_axis=0...  4.26 us
  transfers between devices with their start and end apart: 7, of which 5 were waited for; matrix products, arithmetic and copies ran while one was open for 26% of the time, Pallas kernels for 0%

commit v1 on v0

--- a/solution.py
+++ b/solution.py
@@ -70,7 +70,10 @@
     )
     queries_local, grads_local = (
         lax.all_to_all(query_rows, "sp", split_axis=1, concat_axis=0, tiled=True),
-        lax.all_to_all(out_grad, "sp", split_axis=1, concat_axis=0, tiled=True),
+        jnp.concatenate(
+            lax.all_to_all(jnp.stack(jnp.split(out_grad, lax.axis_size("sp"), axis=1)), "sp", 0, 0),
+            axis=0,
+        ),
     )
     key_heads = KVH * copies // devices
     per_group = QH // devices // key_heads

time: 118 us -> 114 us (0.966)
  local copies, waits for them, and re-layouts: 21.7 us -> 19.8 us
  waiting for transfers between devices: 44 us -> 42.2 us
  matrix products: 21 us -> 19.7 us
    all_to_all x1, waiting for transfers between devices: 11.9 us -> 7.36 us  [on_device(): lax.all_to_all(query_rows, 'sp', split_axis=1, concat_axis=0, tiled=True)]
    another operation x0 -> x3, local copies, waits for them, and re-layouts: none -> 2.97 us  [the longest x2 1.71 us: on_device(): grads = grads_local.reshape(length, key_heads, per_group, HD)]
    dot_general x1, matrix products: 5.91 us -> 3.15 us  [weighted_values(): jnp.einsum('kgbs,skd->bkgd', probs_b, value_block, preferred_element_type...]
    all_to_all x1 -> x0, local copies, waits for them, and re-layouts: 2.29 us -> none  [on_device(): lax.all_to_all(out_grad, 'sp', split_axis=1, concat_axis=0, tiled=True)]
    dot_general x1, matrix products: 1.24 us -> 3.43 us  [backward_block(): jnp.einsum('kgbs,bkgd->skd', score_grad, query_block, preferred_element_t...]
    unnamed x13 -> x15, local copies, waits for them, and re-layouts: 4.96 us -> 3.04 us
    all_to_all x1, waiting for transfers between devices: 11.8 us -> 13.1 us  [on_device(): lax.all_to_all(jnp.stack(jnp.split(out_grad, lax.axis_size('sp'), axis=1)...]
    all_to_all x1, local copies, waits for them, and re-layouts: 2.29 us -> 1.06 us  [on_device(): lax.all_to_all(query_rows, 'sp', split_axis=1, concat_axis=0, tiled=True)]
  transfers between devices with their start and end apart: 7 -> 7, of which waited for: 5 -> 6; matrix products, arithmetic and copies ran while one was open for 26% -> 20% of each run, Pallas kernels for 0% -> 0%
where the time goes in v1:
time: 114 us; the launch traced here: 113 us
  waiting for transfers between devices  42.2 us (37%)
  starting transfers between devices  25.9 us (23%)
  local copies, waits for them, and re-layouts  19.8 us (17%)
  matrix products  19.7 us (17%)
  other arithmetic  5.01 us (4%)
    all_to_all x1, waiting for transfers between devices, on_device(): lax.all_to_all(jnp.stack(jnp.split(out_grad, lax.axis_size('sp'), axis=1)...  13.1 us
    all_to_all x1, waiting for transfers between devices, on_device(): lax.all_to_all(query_local, 'sp', split_axis=0, concat_axis=1, tiled=True)  12.5 us
    all_to_all x1, waiting for transfers between devices, on_device(): lax.all_to_all(query_rows, 'sp', split_axis=1, concat_axis=0, tiled=True)  7.36 us
    all_to_all x1, waiting for transfers between devices, on_device(): lax.all_to_all(widen(key_rows, copies), 'sp', split_axis=1, concat_axis=0...  4.34 us
    all_to_all x1, starting transfers between devices, on_device(): lax.all_to_all(widen(key_rows, copies), 'sp', split_axis=1, concat_axis=0...  4.26 us
    dot_general x1, matrix products, backward_block(): jnp.einsum('bkgd,skd->kgbs', grad_block, value_block, preferred_element_t...  4.1 us
    all_to_all x1, starting transfers between devices, on_device(): lax.all_to_all(widen(value_rows, copies), 'sp', split_axis=1, concat_axis...  4.04 us
    dot_general x1, matrix products, backward_block(): jnp.einsum('kgbs,skd->bkgd', score_grad, key_block, preferred_element_typ...  3.93 us
  transfers between devices with their start and end apart: 7, of which 6 were waited for; matrix products, arithmetic and copies ran while one was open for 20% of the time, Pallas kernels for 0%

profile of v1, /device:TPU:0, one launch (start us, length us, event | category | flops | bytes accessed | tf_op | source)
XLA Modules:
  0.0 113.4 jit_solution(10422318579550234543)
XLA Ops:
  0.7 1.8 %copy.146 = bf16[16,4,8,256]{3,2,0,1:T(8,128)(2,1)} copy(bf16[16,4,8,256]{3,2,1,0:T(8,128)(2,1)} %bitcast.96) | data formatting | bytes 524288 | tf_op jit(solution)/shard_map/all_to_all | solution.py:68
  2.4 4.3 %all-to-all-start = ((bf16[128,4,256]{2,0,1:T(8,128)(2,1)}), bf16[128,4,256]{2,0,1:T(8,128)(2,1)S(1)}, u32[]{:S(2)}, u32[]{:S(2)}) async-start(bf16[128,4,256]{2,0,1:T(8,128)(2,1)} %bitcast.82), calls=%async_computation | async-start | bytes 524288 | tf_op jit(solution)/shard_map/all_to_all | solution.py:68
  6.7 1.7 %copy.145 = bf16[16,4,8,256]{3,2,0,1:T(8,128)(2,1)} copy(bf16[16,4,8,256]{3,2,1,0:T(8,128)(2,1)} %bitcast.97) | data formatting | bytes 524288 | tf_op jit(solution)/shard_map/all_to_all | solution.py:69
  8.3 4.3 %all-to-all-done = bf16[128,4,256]{2,0,1:T(8,128)(2,1)S(1)} async-done(((bf16[128,4,256]{2,0,1:T(8,128)(2,1)}), bf16[128,4,256]{2,0,1:T(8,128)(2,1)S(1)}, u32[]{:S(2)}, u32[]{:S(2)}) %all-to-all-start) | async-done | bytes 262176 | tf_op jit(solution)/shard_map/all_to_all | solution.py:68
  12.7 4.0 %all-to-all-start.3 = ((bf16[128,4,256]{2,0,1:T(8,128)(2,1)}), bf16[128,4,256]{2,0,1:T(8,128)(2,1)}, u32[]{:S(2)}, u32[]{:S(2)}) async-start(bf16[128,4,256]{2,0,1:T(8,128)(2,1)} %bitcast.81), calls=%async_computation.3 | async-start | bytes 524288 | tf_op jit(solution)/shard_map/all_to_all | solution.py:69
  19.1 3.7 %all-to-all-done.3 = bf16[128,4,256]{2,0,1:T(8,128)(2,1)} async-done(((bf16[128,4,256]{2,0,1:T(8,128)(2,1)}), bf16[128,4,256]{2,0,1:T(8,128)(2,1)}, u32[]{:S(2)}, u32[]{:S(2)}) %all-to-all-start.3) | async-done | bytes 262176 | tf_op jit(solution)/shard_map/all_to_all | solution.py:69
  22.8 3.5 %all-to-all-start.2 = ((bf16[4,128,1024]{2,1,0:T(8,128)(2,1)}), bf16[4,128,1024]{2,1,0:T(8,128)(2,1)S(1)}, u32[]{:S(2)}, u32[]{:S(2)}) async-start(bf16[4,128,1024]{2,1,0:T(8,128)(2,1)} %pad_maximum_fusion), calls=%async_computation.2 | async-start | bytes 2097152 | tf_op jit(solution)/shard_map/all_to_all | solution.py:74
  27.7 13.1 %all-to-all-done.2 = bf16[4,128,1024]{2,1,0:T(8,128)(2,1)S(1)} async-done(((bf16[4,128,1024]{2,1,0:T(8,128)(2,1)}), bf16[4,128,1024]{2,1,0:T(8,128)(2,1)S(1)}, u32[]{:S(2)}, u32[]{:S(2)}) %all-to-all-start.2) | async-done | bytes 1048608 | tf_op jit(solution)/shard_map/all_to_all | solution.py:74
  40.7 3.5 %all-to-all-start.1 = ((bf16[128,4,1024]{2,0,1:T(8,128)(2,1)}), bf16[128,4,1024]{2,0,1:T(8,128)(2,1)S(1)}, u32[]{:S(2)}, u32[]{:S(2)}) async-start(bf16[128,4,1024]{2,0,1:T(8,128)(2,1)} %bitcast.80), calls=%async_computation.1 | async-start | bytes 2097152 | tf_op jit(solution)/shard_map/all_to_all | solution.py:72
  44.5 1.7 %reshape.166 = bf16[512,2,128]{2,1,0:T(2,128)(2,1)} reshape(bf16[4,128,256]{2,1,0:T(8,128)(2,1)} %bitcast.90) | data formatting | bytes 524288 | tf_op jit(solution)/shard_map/reshape | solution.py:82
  46.2 1.7 %reshape.168 = bf16[512,2,128]{2,1,0:T(2,128)(2,1)} reshape(bf16[4,128,256]{2,1,0:T(8,128)(2,1)} %bitcast.12) | data formatting | bytes 524288 | tf_op jit(solution)/shard_map/reshape | solution.py:83
  49.7 1.6 %bitcast_convert_fusion = f32[2,4,512,128]{3,1,0,2:T(4,128)} fusion(bf16[512,2,4,128]{3,2,1,0:T(4,128)(2,1)S(1)} %reshape_reshape.3), kind=kLoop, calls=%fused_computation.18 | loop fusion | flops 524288 | bytes 3145728
  51.3 7.4 %all-to-all-done.1 = bf16[128,4,1024]{2,0,1:T(8,128)(2,1)S(1)} async-done(((bf16[128,4,1024]{2,0,1:T(8,128)(2,1)}), bf16[128,4,1024]{2,0,1:T(8,128)(2,1)S(1)}, u32[]{:S(2)}, u32[]{:S(2)}) %all-to-all-start.1) | async-done | bytes 1048608 | tf_op jit(solution)/shard_map/all_to_all | solution.py:72
  59.4 2.6 %fusion.3 = (f32[2,4,512]{2,1,0:T(4,128)S(1)}, f32[2,512,512,4]{2,1,3,0:T(8,128)S(1)}) fusion(pred[512,512]{0,1:T(8,128)(4,1)S(1)} %fusion.7, bf16[512,2,4,128]{3,2,1,0:T(4,128)(2,1)S(1)} %reshape.167, bf16[512,2,128,1]{2,1,0,3:T(2,128)(2,1)} %bitcast.94), kind=kOutput, calls=%fused_computation.7 | convolution fusion | flops 543158272 | bytes 9977856 | tf_op jit(solution)/shard_map/bkgd,skd->kgbs/dot_general | solution.py:30
  62.0 1.8 %exponential_reduce_fusion = f32[2,4,512]{2,1,0:T(4,128)S(1)} fusion(f32[2,512,512,4]{2,1,3,0:T(8,128)S(1)} %get-tuple-element.17, f32[2,4,512]{2,1,0:T(4,128)S(1)} %get-tuple-element.16, pred[512,512]{0,1:T(8,128)(4,1)S(1)} %fusion.7), kind=kLoop, calls=%fused_computation.5 | loop fusion | flops 8384512 | bytes 8683520 | tf_op jit(solution)/shard_map/reduce_sum | solution.py:113
  63.8 2.5 %convolution_bitcast_fusion = bf16[512,2,128]{0,2,1:T(8,128)(2,1)S(1)} fusion(bf16[512,2,4,128]{0,3,2,1:T(8,128)(2,1)S(1)} %copy.91, f32[2,512,512,4]{2,1,3,0:T(8,128)S(1)} %get-tuple-element.17, f32[2,4,512]{2,1,0:T(4,128)S(1)} %bitcast.102, pred[512,512]{0,1:T(8,128)(4,1)S(1)} %fusion.7), kind=kOutput, calls=%fused_computation.12 | convolution fusion | flops 545259520 | bytes 9977856 | tf_op jit(solution)/shard_map/kgbs,bkgd->skd/dot_general | solution.py:41
  66.3 3.1 %multiply_reduce_fusion = f32[2,4,512]{2,1,0:T(4,128)S(1)} fusion(f32[2,4,512,128]{3,1,0,2:T(4,128)S(1)} %copy-done, bf16[512,2,128,1]{2,1,0,3:T(2,128)(2,1)S(1)} %bitcast.98, f32[2,512,512,4]{2,1,3,0:T(8,128)S(1)} %get-tuple-element.17, f32[2,4,512]{2,1,0:T(4,128)S(1)} %bitcast.103, pred[512,512]{0,1:T(8,128)(4,1)S(1)} %fusion.7), kind=kOutput, calls=%fused_computation.8 | convolution fusion | flops 547352576 | bytes 11042816 | tf_op jit(solution)/shard_map/kgbs,skd->bkgd/dot_general | solution.py:37
  69.5 4.1 %fusion.1 = bf16[2,4,512,512]{2,3,1,0:T(8,128)(2,1)} fusion(f32[2,512,512,4]{2,1,3,0:T(8,128)S(1)} %get-tuple-element.17, f32[2,4,512]{2,1,0:T(4,128)S(1)} %multiply_reduce_fusion, f32[2,4,512]{2,1,0:T(4,128)S(1)} %bitcast.104, pred[512,512]{0,1:T(8,128)(4,1)S(1)} %fusion.7, bf16[512,2,4,128]{0,3,2,1:T(8,128)(2,1)S(1)} %copy.91, ...), kind=kOutput, calls=%fused_computation.2 | convolution fusion | flops 549453824 | bytes 14188544 | tf_op jit(solution)/shard_map/bkgd,skd->kgbs/dot_general | solution.py:44
  74.4 3.6 %all-to-all-start.6 = ((bf16[4,128,256]{1,2,0:T(8,128)(2,1)}), bf16[4,128,256]{1,2,0:T(8,128)(2,1)S(1)}, u32[]{:S(2)}, u32[]{:S(2)}) async-start(bf16[4,128,256]{1,2,0:T(8,128)(2,1)} %copy.93), calls=%async_computation.6 | async-start | bytes 524288 | tf_op jit(solution)/shard_map/all_to_all | solution.py:153
  78.0 3.4 %fusion.6 = bf16[512,2,128]{2,0,1:T(8,128)(2,1)S(1)} fusion(bf16[2,4,512,512]{2,3,1,0:T(8,128)(2,1)} %fusion.1, bf16[512,2,4,128]{3,2,1,0:T(4,128)(2,1)S(1)} %reshape.167), kind=kOutput, calls=%fused_computation.15 | convolution fusion | flops 537133056 | bytes 5505024 | tf_op jit(solution)/shard_map/kgbs,bkgd->skd/dot_general | solution.py:52
  83.8 3.4 %all-to-all-start.5 = ((bf16[4,128,256]{2,1,0:T(8,128)(2,1)}), bf16[4,128,256]{2,1,0:T(8,128)(2,1)S(1)}, u32[]{:S(2)}, u32[]{:S(2)}) async-start(bf16[4,128,256]{2,1,0:T(8,128)(2,1)} %all_to_all.87), calls=%async_computation.5 | async-start | bytes 524288 | tf_op jit(solution)/shard_map/all_to_all | solution.py:152
  87.2 3.9 %fusion.4 = bf16[512,2,4,128]{3,0,2,1:T(8,128)(2,1)S(1)} fusion(bf16[2,4,512,512]{2,3,1,0:T(8,128)(2,1)} %fusion.1, bf16[512,2,128,1]{2,1,0,3:T(2,128)(2,1)S(1)} %bitcast.95), kind=kOutput, calls=%fused_computation.11 | convolution fusion | flops 537919488 | bytes 5505024 | tf_op jit(solution)/shard_map/kgbs,skd->bkgd/dot_general | solution.py:48
  93.5 3.5 %all-to-all-start.4 = ((bf16[4,128,1024]{2,1,0:T(8,128)(2,1)}), bf16[4,128,1024]{2,1,0:T(8,128)(2,1)S(1)}, u32[]{:S(2)}, u32[]{:S(2)}) async-start(bf16[4,128,1024]{2,1,0:T(8,128)(2,1)} %all_to_all.83), calls=%async_computation.4 | async-start | bytes 2097152 | tf_op jit(solution)/shard_map/all_to_all | solution.py:150
  98.9 12.5 %all-to-all-done.4 = bf16[4,128,1024]{2,1,0:T(8,128)(2,1)S(1)} async-done(((bf16[4,128,1024]{2,1,0:T(8,128)(2,1)}), bf16[4,128,1024]{2,1,0:T(8,128)(2,1)S(1)}, u32[]{:S(2)}, u32[]{:S(2)}) %all-to-all-start.4) | async-done | bytes 1048608 | tf_op jit(solution)/shard_map/all_to_all | solution.py:150
  (38 shorter events, 15.8 us)
Async XLA Ops:
  0.6 25.7 %copy-start.1 = (bf16[128,4096]{1,0:T(8,128)(2,1)S(1)}, bf16[128,4096]{1,0:T(8,128)(2,1)}, u32[]{:S(2)}) copy-start(bf16[128,4096]{1,0:T(8,128)(2,1)} %param.5) | copy-start | bytes 3145732
  0.6 26.8 %copy-start.5 = (s32[8]{0:T(128)S(1)}, s32[8]{0:T(128)}, u32[]{:S(2)}) copy-start(s32[8]{0:T(128)} %param.9) | copy-start | bytes 100
  2.4 10.3 %all-to-all-start = ((bf16[128,4,256]{2,0,1:T(8,128)(2,1)}), bf16[128,4,256]{2,0,1:T(8,128)(2,1)S(1)}, u32[]{:S(2)}, u32[]{:S(2)}) async-start(bf16[128,4,256]{2,0,1:T(8,128)(2,1)} %bitcast.82), calls=%async_computation | async-start | bytes 524288 | tf_op jit(solution)/shard_map/all_to_all | solution.py:68
  12.7 10.1 %copy-start.2 = (bf16[128,4,256]{2,0,1:T(8,128)(2,1)}, bf16[128,4,256]{2,0,1:T(8,128)(2,1)S(1)}, u32[]{:S(2)}) copy-start(bf16[128,4,256]{2,0,1:T(8,128)(2,1)S(1)} %all-to-all-done) | copy-start | bytes 786436
  12.7 10.1 %all-to-all-start.3 = ((bf16[128,4,256]{2,0,1:T(8,128)(2,1)}), bf16[128,4,256]{2,0,1:T(8,128)(2,1)}, u32[]{:S(2)}, u32[]{:S(2)}) async-start(bf16[128,4,256]{2,0,1:T(8,128)(2,1)} %bitcast.81), calls=%async_computation.3 | async-start | bytes 524288 | tf_op jit(solution)/shard_map/all_to_all | solution.py:69
  22.8 17.9 %all-to-all-start.2 = ((bf16[4,128,1024]{2,1,0:T(8,128)(2,1)}), bf16[4,128,1024]{2,1,0:T(8,128)(2,1)S(1)}, u32[]{:S(2)}, u32[]{:S(2)}) async-start(bf16[4,128,1024]{2,1,0:T(8,128)(2,1)} %pad_maximum_fusion), calls=%async_computation.2 | async-start | bytes 2097152 | tf_op jit(solution)/shard_map/all_to_all | solution.py:74
  40.7 17.9 %all-to-all-start.1 = ((bf16[128,4,1024]{2,0,1:T(8,128)(2,1)}), bf16[128,4,1024]{2,0,1:T(8,128)(2,1)S(1)}, u32[]{:S(2)}, u32[]{:S(2)}) async-start(bf16[128,4,1024]{2,0,1:T(8,128)(2,1)} %bitcast.80), calls=%async_computation.1 | async-start | bytes 2097152 | tf_op jit(solution)/shard_map/all_to_all | solution.py:72
  63.8 2.5 %copy-start = (f32[2,4,512,128]{3,1,0,2:T(4,128)S(1)}, f32[2,4,512,128]{3,1,0,2:T(4,128)}, u32[]{:S(2)}) copy-start(f32[2,4,512,128]{3,1,0,2:T(4,128)} %bitcast_convert_fusion) | copy-start | bytes 6291460
  63.8 2.5 %copy-start.4 = (bf16[512,2,128]{2,1,0:T(2,128)(2,1)S(1)}, bf16[512,2,128]{2,1,0:T(2,128)(2,1)}, u32[]{:S(2)}) copy-start(bf16[512,2,128]{2,1,0:T(2,128)(2,1)} %reshape.168) | copy-start | bytes 786436
  73.6 13.6 %copy-start.3 = (bf16[512,2,128]{2,1,0:T(2,128)(2,1)S(1)}, bf16[512,2,128]{2,1,0:T(2,128)(2,1)}, u32[]{:S(2)}) copy-start(bf16[512,2,128]{2,1,0:T(2,128)(2,1)} %reshape.166) | copy-start | bytes 786436
  74.4 9.4 %all-to-all-start.6 = ((bf16[4,128,256]{1,2,0:T(8,128)(2,1)}), bf16[4,128,256]{1,2,0:T(8,128)(2,1)S(1)}, u32[]{:S(2)}, u32[]{:S(2)}) async-start(bf16[4,128,256]{1,2,0:T(8,128)(2,1)} %copy.93), calls=%async_computation.6 | async-start | bytes 524288 | tf_op jit(solution)/shard_map/all_to_all | solution.py:153
  83.8 9.7 %all-to-all-start.5 = ((bf16[4,128,256]{2,1,0:T(8,128)(2,1)}), bf16[4,128,256]{2,1,0:T(8,128)(2,1)S(1)}, u32[]{:S(2)}, u32[]{:S(2)}) async-start(bf16[4,128,256]{2,1,0:T(8,128)(2,1)} %all_to_all.87), calls=%async_computation.5 | async-start | bytes 524288 | tf_op jit(solution)/shard_map/all_to_all | solution.py:152
  93.5 17.9 %all-to-all-start.4 = ((bf16[4,128,1024]{2,1,0:T(8,128)(2,1)}), bf16[4,128,1024]{2,1,0:T(8,128)(2,1)S(1)}, u32[]{:S(2)}, u32[]{:S(2)}) async-start(bf16[4,128,1024]{2,1,0:T(8,128)(2,1)} %all_to_all.83), calls=%async_computation.4 | async-start | bytes 2097152 | tf_op jit(solution)/shard_map/all_to_all | solution.py:150
